TPU v7x, 256 devices: a whole 4x4x8 slice. The times are simulated.
256 devices in a mesh: copy: 2 (over core), fsdp: 32 (over z, y), tp: 4 (over x).
Axes of the slice: x: 4, y: 4, z: 8, core: 2. Of those that a mesh axis runs over, the one named last changes fastest.
Arguments:
- gradients: float32 [256, 128, 4096], P('copy', 'fsdp', 'tp'), parts along dimension 0, may hold values from -6 to 6
- momentum: float32 [256, 128, 4096], P('copy', 'fsdp', 'tp'), parts along dimension 0, may hold values from -6 to 6
- weights: float32 [256, 128, 4096], P('copy', 'fsdp', 'tp'), parts along dimension 0, may hold values from -0.1875 to 0.1875
Outputs:
- new_weights: float32 [256, 128, 4096], P('copy', 'fsdp', 'tp'), parts along dimension 0
- new_momentum: float32 [256, 128, 4096], P('copy', 'fsdp', 'tp'), parts along dimension 0
There are 2 independent parts, one for each index of `copy`. A program takes and returns all parts, laid end to end along the dimension named above; each array names one. Nothing has to cross between parts.
All inputs are finite; a program needn't handle non-finite values.
Results may differ from a plain program's by a relative error of at most 0.00014.
Values sent between devices are 32-bit elements; how exact they have to be, the bound alone decides.
A program may use at most 64 MiB of HBM per device.

v0:
```python
import jax
import jax.numpy as jnp
from jax import lax
from jax.sharding import PartitionSpec as P

ITERS = 4
hold_rate = 0.95
learn_rate = 0.9
decay_rate = 0.1


def sent_to_all(x, axis):
    length = lax.axis_size(axis)
    return lax.all_to_all(jnp.broadcast_to(x[None], (length, *x.shape)), axis, 0, 0, tiled=True)


def taken_together(x, axis):
    return sent_to_all(x, axis).sum(axis=0)


def shards(gradients, momentum, weights):
    new_momentum = hold_rate * momentum + gradients
    direction = hold_rate * new_momentum + gradients
    moved = lax.all_to_all(direction, "fsdp", split_axis=0, concat_axis=1, tiled=True)
    total = lax.psum(jnp.sum(moved * moved, axis=(1, 2), keepdims=True), "tp")
    iterate = moved * lax.rsqrt(total + 1e-06)
    for step in range(ITERS):
        gram = taken_together(
            jnp.einsum("mik,mjk->mij", iterate, iterate, precision=lax.Precision.HIGHEST), "tp"
        )
        mixed = -4.775 * gram + 2.0315 * jnp.einsum(
            "mij,mjk->mik", gram, gram, precision=lax.Precision.HIGHEST
        )
        iterate = 3.4445 * iterate + jnp.einsum(
            "mij,mjk->mik", mixed, iterate, precision=lax.Precision.HIGHEST
        )
    back = lax.all_to_all(iterate, "fsdp", split_axis=1, concat_axis=0, tiled=True)
    new_weights = (1.0 - learn_rate * decay_rate) * weights - learn_rate * back
    return (new_weights, new_momentum)


def solution(mesh):
    return jax.shard_map(
        shards,
        mesh=mesh,
        in_specs=(P("copy", "fsdp", "tp"), P("copy", "fsdp", "tp"), P("copy", "fsdp", "tp")),
        out_specs=(P("copy", "fsdp", "tp"), P("copy", "fsdp", "tp")),
        check_vma=False,
    )
```

profile of v0, /device:TPU:8, one launch (start us, length us, event | category | flops | bytes accessed | tf_op | source)
XLA Modules:
  0.0 217.4 jit_solution(7391377207697536260)
XLA Ops:
  0.6 4.6 %multiply_add_fusion.4 = (f32[128,4,1024]{2,1,0:T(4,128)S(1)}, f32[128,4,1024]{2,1,0:T(4,128)}) fusion(f32[128,4,1024]{2,1,0:T(4,128)} %param.3, f32[128,4,1024]{2,1,0:T(4,128)} %param.4), kind=kLoop, calls=%fused_computation.7 | loop fusion | flops 2097152 | bytes 8388608 | tf_op jit(solution)/shard_map/add | solution.py:23
  5.3 62.0 %all_to_all.47 = f32[128,4,1024]{2,1,0:T(4,128)S(1)} all-to-all(f32[128,4,1024]{2,1,0:T(4,128)S(1)} %get-tuple-element.2), channel_id=1, replica_groups=mesh['copy'=2,'fsdp'=32,'tp'=4] {'fsdp'}, dimensions={0} | all-to-all | bytes 4194304 | tf_op jit(solution)/shard_map/all_to_all | solution.py:24
  67.3 0.6 multiply_reduce_fusion
  67.9 10.5 %psum.7 = f32[4,1,1]{0,2,1:T(1,128)S(1)} all-reduce(f32[4,1,1]{0,2,1:T(1,128)S(1)} %bitcast.38), channel_id=1, replica_groups=mesh['copy'=2,'fsdp'=32,'tp'=4] {'tp'}, use_global_device_ids=true, to_apply=%region_1.0 | all-reduce | flops 4 | bytes 32 | tf_op jit(solution)/shard_map/psum | solution.py:25
  78.4 1.5 copy_bitcast_fusion
  79.9 2.0 all_to_all.35
  81.9 0.0 copy-start.1
  81.9 2.3 %fusion.2 = f32[4,128,128]{2,1,0:T(8,128)S(1)} fusion(f32[4,128,1024]{2,1,0:T(8,128)S(1)} %all_to_all.35, f32[4]{0:T(128)S(1)} %rsqrt_bitcast_fusion), kind=kOutput, calls=%fused_computation.11 | convolution fusion | flops 805830656 | bytes 2359312 | tf_op jit(solution)/shard_map/mik,mjk->mij/dot_general | solution.py:29
  84.2 0.1 broadcast_in_dim.11
  84.3 14.1 %all_to_all.48 = f32[4,4,128,128]{3,2,1,0:T(8,128)S(1)} all-to-all(f32[4,4,128,128]{3,2,1,0:T(8,128)S(1)} %broadcast_in_dim.11), channel_id=1, replica_groups=mesh['copy'=2,'fsdp'=32,'tp'=4] {'tp'}, dimensions={0} | all-to-all | bytes 2097152 | tf_op jit(solution)/shard_map/all_to_all | solution.py:14
  98.4 0.0 copy-done.1
  98.4 0.1 reduce_sum.46
  98.5 0.4 fusion.9
  98.8 4.3 %multiply_add_fusion.3 = f32[4,128,1024]{2,1,0:T(8,128)S(1)} fusion(f32[4,128,1024]{2,1,0:T(8,128)} %copy-done.1, f32[4,128,128]{2,1,0:T(8,128)S(1)} %fusion.9, f32[4]{0:T(128)S(1)} %rsqrt_bitcast_fusion), kind=kOutput, calls=%fused_computation.5 | convolution fusion | flops 807403520 | bytes 4456464 | tf_op jit(solution)/shard_map/mij,mjk->mik/dot_general | solution.py:34
  103.1 2.0 fusion.12
  105.2 0.1 broadcast_in_dim.12
  105.3 13.3 %all_to_all.49 = f32[4,4,128,128]{3,2,1,0:T(8,128)S(1)} all-to-all(f32[4,4,128,128]{3,2,1,0:T(8,128)S(1)} %broadcast_in_dim.12), channel_id=1, replica_groups=mesh['copy'=2,'fsdp'=32,'tp'=4] {'tp'}, dimensions={0} | all-to-all | bytes 2097152 | tf_op jit(solution)/shard_map/all_to_all | solution.py:14
  118.6 0.1 reduce_sum.47
  118.7 0.4 fusion.8
  119.0 2.0 multiply_add_fusion.2
  121.1 0.0 copy-start
  121.1 2.0 fusion.13
  123.2 0.0 copy-done
  123.2 0.1 broadcast_in_dim.13
  123.3 13.3 %all_to_all.50 = f32[4,4,128,128]{3,2,1,0:T(8,128)S(1)} all-to-all(f32[4,4,128,128]{3,2,1,0:T(8,128)S(1)} %broadcast_in_dim.13), channel_id=1, replica_groups=mesh['copy'=2,'fsdp'=32,'tp'=4] {'tp'}, dimensions={0} | all-to-all | bytes 2097152 | tf_op jit(solution)/shard_map/all_to_all | solution.py:14
  136.6 0.1 reduce_sum.48
  136.7 0.4 fusion.7
  137.0 4.2 %multiply_add_fusion.1 = f32[4,128,1024]{2,1,0:T(8,128)S(1)} fusion(f32[4,128,1024]{2,1,0:T(8,128)} %copy-done, f32[4,128,128]{2,1,0:T(8,128)S(1)} %fusion.7), kind=kOutput, calls=%fused_computation.3 | convolution fusion | flops 806354944 | bytes 4456448 | tf_op jit(solution)/shard_map/mij,mjk->mik/dot_general | solution.py:34
  141.2 2.0 fusion.14
  143.3 0.1 broadcast_in_dim.14
  143.4 13.3 %all_to_all.51 = f32[4,4,128,128]{3,2,1,0:T(8,128)S(1)} all-to-all(f32[4,4,128,128]{3,2,1,0:T(8,128)S(1)} %broadcast_in_dim.14), channel_id=1, replica_groups=mesh['copy'=2,'fsdp'=32,'tp'=4] {'tp'}, dimensions={0} | all-to-all | bytes 2097152 | tf_op jit(solution)/shard_map/all_to_all | solution.py:14
  156.7 0.1 reduce_sum.49
  156.8 0.4 fusion.6
  157.1 2.0 multiply_add_fusion
  159.2 1.4 copy.11
  160.5 51.9 %all_to_all.52 = f32[4,128,1024]{2,0,1:T(4,128)S(1)} all-to-all(f32[4,128,1024]{2,0,1:T(4,128)S(1)} %copy.11), channel_id=1, replica_groups=mesh['copy'=2,'fsdp'=32,'tp'=4] {'fsdp'}, dimensions={1} | all-to-all | bytes 4194304 | tf_op jit(solution)/shard_map/all_to_all | solution.py:37
  212.4 0.7 broadcast_multiply_fusion
  213.1 0.0 copy-start.2
  213.1 1.8 copy.12
  214.9 0.0 copy-done.2
  214.9 2.5 %bitcast_subtract_fusion = f32[128,4,1024]{2,1,0:T(4,128)} fusion(f32[32,4,4,1024]{3,2,1,0:T(4,128)S(1)} %copy.12, f32[128,4,1024]{2,1,0:T(4,128)S(1)} %copy-done.2), kind=kLoop, calls=%fused_computation | loop fusion | flops 1048576 | bytes 6291456 | tf_op jit(solution)/shard_map/sub | solution.py:38
  (1 shorter events, 0.0 us)
Async XLA Ops:
  81.9 16.5 %copy-start.1 = (f32[4,128,1024]{2,1,0:T(8,128)}, f32[4,128,1024]{2,1,0:T(8,128)S(1)}, u32[]{:S(2)}) copy-start(f32[4,128,1024]{2,1,0:T(8,128)S(1)} %all_to_all.35) | copy-start | bytes 6291460
  121.1 2.1 copy-start
  213.1 1.8 copy-start.2
where the time goes:
time: 218 us; the launch traced here: 217 us
  blocking collectives  178 us (82%)
  matrix products  22.4 us (10%)
  other arithmetic  8.7 us (4%)
  local copies, waits for them, and re-layouts  7.09 us (3%)
    all_to_all x1, blocking collectives, shards(): lax.all_to_all(direction, 'fsdp', split_axis=0, concat_axis=1, tiled=True)  62 us
    all_to_all x4, blocking collectives, sent_to_all(): lax.all_to_all(jnp.broadcast_to(x[None], (length, *x.shape)), axis, 0, 0,...  54 us
    all_to_all x1, blocking collectives, shards(): lax.all_to_all(iterate, 'fsdp', split_axis=1, concat_axis=0, tiled=True)  51.9 us
    dot_general x4, matrix products, shards(): jnp.einsum('mij,mjk->mik', mixed, iterate, precision=lax.Precision.HIGHEST)  12.5 us
    psum x1, blocking collectives, shards(): total = lax.psum(jnp.sum(moved * moved, axis=(1, 2), keepdims=True), 'tp')  10.5 us
    dot_general x4, matrix products, shards(): jnp.einsum('mik,mjk->mij', iterate, iterate, precision=lax.Precision.HIGH...  8.4 us
    add x1, other arithmetic, shards(): direction = hold_rate * new_momentum + gradients  4.62 us

commit v1 on v0

--- a/solution.py
+++ b/solution.py
@@ -34,7 +34,12 @@
         iterate = 3.4445 * iterate + jnp.einsum(
             "mij,mjk->mik", mixed, iterate, precision=lax.Precision.HIGHEST
         )
-    back = lax.all_to_all(iterate, "fsdp", split_axis=1, concat_axis=0, tiled=True)
+    back = jnp.concatenate(
+        lax.all_to_all(
+            jnp.stack(jnp.split(iterate, lax.psum(1, "fsdp"), axis=1), axis=0), "fsdp", 0, 0
+        ),
+        axis=0,
+    )
     new_weights = (1.0 - learn_rate * decay_rate) * weights - learn_rate * back
     return (new_weights, new_momentum)
 

time: 218 us -> 216 us (level)
  no operation moved by 1% of the time
where the time goes in v1:
time: 216 us
  blocking collectives  178 us (82%)
  matrix products  22.4 us (10%)
  other arithmetic  8.6 us (4%)
  local copies, waits for them, and re-layouts  5.61 us (3%)
    all_to_all x1, blocking collectives, shards(): lax.all_to_all(direction, 'fsdp', split_axis=0, concat_axis=1, tiled=True)  62 us
    all_to_all x4, blocking collectives, sent_to_all(): lax.all_to_all(jnp.broadcast_to(x[None], (length, *x.shape)), axis, 0, 0,...  54 us
    all_to_all x1, blocking collectives, shards(): lax.all_to_all(jnp.stack(jnp.split(iterate, lax.psum(1, 'fsdp'), axis=1),...  51.9 us
    dot_general x4, matrix products, shards(): jnp.einsum('mij,mjk->mik', mixed, iterate, precision=lax.Precision.HIGHEST)  12.5 us
    psum x1, blocking collectives, shards(): total = lax.psum(jnp.sum(moved * moved, axis=(1, 2), keepdims=True), 'tp')  10.5 us
    dot_general x4, matrix products, shards(): jnp.einsum('mik,mjk->mij', iterate, iterate, precision=lax.Precision.HIGH...  8.4 us
    add x1, other arithmetic, shards(): direction = hold_rate * new_momentum + gradients  4.62 us

profile of v1, /device:TPU:8, one launch (start us, length us, event | category | flops | bytes accessed | tf_op | source)
XLA Modules:
  0.0 216.0 jit_solution(4196963520418748703)
XLA Ops:
  0.6 4.6 %multiply_add_fusion.4 = (f32[128,4,1024]{2,1,0:T(4,128)S(1)}, f32[128,4,1024]{2,1,0:T(4,128)}) fusion(f32[128,4,1024]{2,1,0:T(4,128)} %param.3, f32[128,4,1024]{2,1,0:T(4,128)} %param.4), kind=kLoop, calls=%fused_computation.7 | loop fusion | flops 2097152 | bytes 8388608 | tf_op jit(solution)/shard_map/add | solution.py:23
  5.3 62.0 %all_to_all.43 = f32[128,4,1024]{2,1,0:T(4,128)S(1)} all-to-all(f32[128,4,1024]{2,1,0:T(4,128)S(1)} %get-tuple-element.2), channel_id=1, replica_groups=mesh['copy'=2,'fsdp'=32,'tp'=4] {'fsdp'}, dimensions={0} | all-to-all | bytes 4194304 | tf_op jit(solution)/shard_map/all_to_all | solution.py:24
  67.3 0.6 multiply_reduce_fusion
  67.9 10.5 %psum.7 = f32[4,1,1]{0,2,1:T(1,128)S(1)} all-reduce(f32[4,1,1]{0,2,1:T(1,128)S(1)} %bitcast.162), channel_id=1, replica_groups=mesh['copy'=2,'fsdp'=32,'tp'=4] {'tp'}, use_global_device_ids=true, to_apply=%region_1.0 | all-reduce | flops 4 | bytes 32 | tf_op jit(solution)/shard_map/psum | solution.py:25
  78.4 1.5 copy_bitcast_fusion
  79.9 2.0 all_to_all.31
  81.9 0.0 copy-start.1
  81.9 2.3 %fusion.2 = f32[4,128,128]{2,1,0:T(8,128)S(1)} fusion(f32[4,128,1024]{2,1,0:T(8,128)S(1)} %all_to_all.31, f32[4]{0:T(128)S(1)} %rsqrt_bitcast_fusion), kind=kOutput, calls=%fused_computation.11 | convolution fusion | flops 805830656 | bytes 2359312 | tf_op jit(solution)/shard_map/mik,mjk->mij/dot_general | solution.py:29
  84.2 0.1 broadcast_in_dim.11
  84.3 14.1 %all_to_all.44 = f32[4,4,128,128]{3,2,1,0:T(8,128)S(1)} all-to-all(f32[4,4,128,128]{3,2,1,0:T(8,128)S(1)} %broadcast_in_dim.11), channel_id=1, replica_groups=mesh['copy'=2,'fsdp'=32,'tp'=4] {'tp'}, dimensions={0} | all-to-all | bytes 2097152 | tf_op jit(solution)/shard_map/all_to_all | solution.py:14
  98.4 0.0 copy-done.1
  98.4 0.1 reduce_sum.46
  98.5 0.4 fusion.9
  98.8 4.3 %multiply_add_fusion.3 = f32[4,128,1024]{2,1,0:T(8,128)S(1)} fusion(f32[4,128,1024]{2,1,0:T(8,128)} %copy-done.1, f32[4,128,128]{2,1,0:T(8,128)S(1)} %fusion.9, f32[4]{0:T(128)S(1)} %rsqrt_bitcast_fusion), kind=kOutput, calls=%fused_computation.5 | convolution fusion | flops 807403520 | bytes 4456464 | tf_op jit(solution)/shard_map/mij,mjk->mik/dot_general | solution.py:34
  103.1 2.0 fusion.12
  105.2 0.1 broadcast_in_dim.12
  105.3 13.3 %all_to_all.45 = f32[4,4,128,128]{3,2,1,0:T(8,128)S(1)} all-to-all(f32[4,4,128,128]{3,2,1,0:T(8,128)S(1)} %broadcast_in_dim.12), channel_id=1, replica_groups=mesh['copy'=2,'fsdp'=32,'tp'=4] {'tp'}, dimensions={0} | all-to-all | bytes 2097152 | tf_op jit(solution)/shard_map/all_to_all | solution.py:14
  118.6 0.1 reduce_sum.47
  118.7 0.4 fusion.8
  119.0 2.0 multiply_add_fusion.2
  121.1 0.0 copy-start
  121.1 2.0 fusion.13
  123.2 0.0 copy-done
  123.2 0.1 broadcast_in_dim.13
  123.3 13.3 %all_to_all.46 = f32[4,4,128,128]{3,2,1,0:T(8,128)S(1)} all-to-all(f32[4,4,128,128]{3,2,1,0:T(8,128)S(1)} %broadcast_in_dim.13), channel_id=1, replica_groups=mesh['copy'=2,'fsdp'=32,'tp'=4] {'tp'}, dimensions={0} | all-to-all | bytes 2097152 | tf_op jit(solution)/shard_map/all_to_all | solution.py:14
  136.6 0.1 reduce_sum.48
  136.7 0.4 fusion.7
  137.0 4.2 %multiply_add_fusion.1 = f32[4,128,1024]{2,1,0:T(8,128)S(1)} fusion(f32[4,128,1024]{2,1,0:T(8,128)} %copy-done, f32[4,128,128]{2,1,0:T(8,128)S(1)} %fusion.7), kind=kOutput, calls=%fused_computation.3 | convolution fusion | flops 806354944 | bytes 4456448 | tf_op jit(solution)/shard_map/mij,mjk->mik/dot_general | solution.py:34
  141.2 2.0 fusion.14
  143.3 0.1 broadcast_in_dim.14
  143.4 13.3 %all_to_all.47 = f32[4,4,128,128]{3,2,1,0:T(8,128)S(1)} all-to-all(f32[4,4,128,128]{3,2,1,0:T(8,128)S(1)} %broadcast_in_dim.14), channel_id=1, replica_groups=mesh['copy'=2,'fsdp'=32,'tp'=4] {'tp'}, dimensions={0} | all-to-all | bytes 2097152 | tf_op jit(solution)/shard_map/all_to_all | solution.py:14
  156.7 0.1 reduce_sum.49
  156.8 0.4 fusion.6
  157.1 2.0 multiply_add_fusion
  160.0 51.9 %all_to_all.48 = f32[32,4,4,1024]{3,2,1,0:T(4,128)S(1)} all-to-all(f32[32,4,4,1024]{3,2,1,0:T(4,128)S(1)} %constant_dynamic-update-slice_fusion), channel_id=1, replica_groups=mesh['copy'=2,'fsdp'=32,'tp'=4] {'fsdp'}, dimensions={0} | all-to-all | bytes 4194304 | tf_op jit(solution)/shard_map/all_to_all | solution.py:38
  211.9 0.0 copy-start.2
  211.9 0.6 broadcast_multiply_fusion
  212.5 1.0 copy-done.2
  213.5 2.5 %bitcast_subtract_fusion = f32[128,4,1024]{2,1,0:T(4,128)} fusion(f32[32,4,4,1024]{3,2,1,0:T(4,128)S(1)} %broadcast_multiply_fusion, f32[128,4,1024]{2,1,0:T(4,128)S(1)} %copy-done.2), kind=kLoop, calls=%fused_computation | loop fusion | flops 1048576 | bytes 6291456 | tf_op jit(solution)/shard_map/sub | solution.py:43
  (33 shorter events, 0.7 us)
Async XLA Ops:
  81.9 16.5 %copy-start.1 = (f32[4,128,1024]{2,1,0:T(8,128)}, f32[4,128,1024]{2,1,0:T(8,128)S(1)}, u32[]{:S(2)}) copy-start(f32[4,128,1024]{2,1,0:T(8,128)S(1)} %all_to_all.31) | copy-start | bytes 6291460
  121.1 2.1 copy-start
  211.9 1.6 copy-start.2
